TPU v7x, 32 devices: a whole 2x2x4 slice. The times are simulated.
32 devices in a mesh: gz: 8 (over z, y), xy: 4 (over x, core).
Axes of the slice: x: 2, y: 2, z: 4, core: 2. Of those that a mesh axis runs over, the one named last changes fastest.
Arguments:
- image: float32 [64, 512, 512], P('gz', 'xy'), may hold values from -6 to 6
- offsets: int32 [4, 64, 4, 4], P(None, 'gz', 'xy'), may hold values from -6 to 6
- frac_index: int32 [4, 64, 4, 4], P(None, 'gz', 'xy'), may hold values from 0 to 15
- fractions: float32 [16, 3], replicated, may hold values from 0 to 1
Outputs:
- transported: float32 [64, 512, 512], P('gz', 'xy')
All inputs are finite; a program needn't handle non-finite values.
Results may differ from a plain program's by a relative error of at most 0.0003.
Values sent between devices are 32-bit elements; how exact they have to be, the bound alone decides.
A program may use at most 128 MiB of HBM per device.

v0:
```python
import jax
import jax.numpy as jnp
from jax import lax
from jax.sharding import PartitionSpec as P


def extended(cells, sides, width):
    for axis, dim in sides:
        count = lax.axis_size(axis)
        head = lax.slice_in_dim(cells, 0, width, axis=dim)
        tail = lax.slice_in_dim(cells, cells.shape[dim] - width, cells.shape[dim], axis=dim)
        cells = jnp.concatenate(
            [
                lax.ppermute(tail, axis, [(i, (i + 1) % count) for i in range(count)]),
                cells,
                lax.ppermute(head, axis, [((i + 1) % count, i) for i in range(count)]),
            ],
            axis=dim,
        )
    return cells


def cubic_weights(shares):
    return (
        -shares * (shares - 1.0) * (shares - 2.0) / 6.0,
        (shares + 1.0) * (shares - 1.0) * (shares - 2.0) / 2.0,
        -(shares + 1.0) * shares * (shares - 2.0) / 2.0,
        (shares + 1.0) * shares * (shares - 1.0) / 6.0,
    )


def column_steps(image, offsets, frac_index, fractions):
    step_count = offsets.shape[0]
    all_shifts, all_index = (
        lax.all_gather(offsets, "gz", axis=1, tiled=True),
        lax.all_gather(frac_index, "gz", axis=1, tiled=True),
    )
    standing = jnp.swapaxes(
        lax.all_to_all(image, "gz", split_axis=2, concat_axis=0, tiled=True), 1, 2
    )
    total_planes = standing.shape[0]
    width_y = standing.shape[1]
    width_x = standing.shape[2]
    column_block = lax.axis_index("gz") * width_y // width_x
    block_pick = (jnp.arange(all_shifts.shape[3], dtype=jnp.int32) == column_block).astype(
        jnp.int32
    )
    levels = jnp.arange(total_planes, dtype=jnp.int32)
    table_rows = jnp.arange(fractions.shape[0], dtype=jnp.int32)
    for step_index in range(step_count):
        shifts_now = jnp.sum(all_shifts[step_index, :, 0, :] * block_pick[None, :], axis=1)
        index_now = jnp.sum(all_index[step_index, :, 0, :] * block_pick[None, :], axis=1)
        onehot = (index_now[:, None] == table_rows[None, :]).astype(jnp.float32)
        picked = jnp.dot(onehot, fractions, precision=lax.Precision.HIGHEST)
        zweights = cubic_weights(1.0 - picked[:, 0])
        xweights = cubic_weights(1.0 - picked[:, 1])
        yweights = cubic_weights(1.0 - picked[:, 2])
        rimmed = extended(standing, (("gz", 1), ("xy", 2)), 2)
        merged = jnp.zeros(rimmed.shape, jnp.float32)
        for node in range(4):
            source = jnp.mod(levels - shifts_now - 2 + node, total_planes)
            merged = merged + zweights[node][:, None, None] * jnp.take(rimmed, source, axis=0)
        along_y = jnp.zeros((total_planes, width_y, width_x + 4), jnp.float32)
        for node in range(4):
            along_y = along_y + yweights[node][:, None, None] * merged[:, node : node + width_y, :]
        along_x = jnp.zeros((total_planes, width_y, width_x), jnp.float32)
        for node in range(4):
            along_x = along_x + xweights[node][:, None, None] * along_y[:, :, node : node + width_x]
        standing = along_x
    return lax.all_to_all(
        jnp.swapaxes(standing, 1, 2), "gz", split_axis=0, concat_axis=2, tiled=True
    )


def local(image, offsets, frac_index, fractions):
    return column_steps(image, offsets, frac_index, fractions)


def solution(mesh):
    in_specs = (P("gz", "xy", None), P(None, "gz", "xy", None), P(None, "gz", "xy", None), P())
    out_specs = P("gz", "xy", None)
    return jax.shard_map(local, mesh=mesh, in_specs=in_specs, out_specs=out_specs, check_vma=False)
```

profile of v0, /device:TPU:0, one launch (start us, length us, event | category | flops | bytes accessed | tf_op | source)
XLA Modules:
  0.0 443.4 jit_solution(4297421122283835696)
XLA Ops:
  2.9 7.3 %all-to-all-start = ((f32[8,128,512]{1,0,2:T(8,128)}), f32[8,128,512]{1,0,2:T(8,128)S(1)}, u32[]{:S(2)}, u32[]{:S(2)}) async-start(f32[8,128,512]{1,0,2:T(8,128)} %copy.20), calls=%async_computation | async-start | bytes 4194304 | tf_op jit(solution)/shard_map/all_to_all | solution.py:39
  10.5 68.2 %all_gather.6 = s32[4,64,1,4]{3,0,2,1:T(4,128)S(1)} all-gather(s32[4,8,1,4]{3,0,2,1:T(4,128)S(1)} %copy.11), channel_id=1, replica_groups=mesh['gz'=8,'xy'=4] {'gz'}, dimensions={1}, use_global_device_ids=true | all-gather | bytes 4608 | tf_op jit(solution)/shard_map/all_gather | solution.py:36
  78.7 30.5 %all_gather.7 = s32[4,64,1,4]{3,0,2,1:T(4,128)S(1)} all-gather(s32[4,8,1,4]{3,0,2,1:T(4,128)S(1)} %copy.13), channel_id=1, replica_groups=mesh['gz'=8,'xy'=4] {'gz'}, dimensions={1}, use_global_device_ids=true | all-gather | bytes 4608 | tf_op jit(solution)/shard_map/all_gather | solution.py:35
  118.0 8.1 %fusion.160 = (f32[64,2,128]{1,2,0:T(8,128)}, f32[64,2,128]{1,2,0:T(8,128)}) fusion(f32[64,64,128]{1,2,0:T(8,128)} %bitcast.517), kind=kLoop, calls=%fused_computation.473 | loop fusion | bytes 262144 | tf_op jit(solution)/shard_map/slice | solution.py:11
  151.9 5.2 %gather_fusion = f32[64,68,132]{1,2,0:T(8,128)} fusion(f32[64,68,132]{1,2,0:T(8,128)} %pad_maximum_fusion, s32[1024]{0:T(1024)S(1)} %get-tuple-element.145), kind=kCustom, calls=%fused_computation.clone | custom fusion | bytes 4595968 | tf_op jit(solution)/shard_map/jit(_take)/gather | solution.py:62
  157.1 5.1 %gather_fusion.1 = f32[64,68,132]{1,2,0:T(8,128)} fusion(f32[64,68,132]{1,2,0:T(8,128)} %pad_maximum_fusion, s32[1024]{0:T(1024)S(1)} %get-tuple-element.144), kind=kCustom, calls=%fused_computation.1.clone | custom fusion | bytes 4595968 | tf_op jit(solution)/shard_map/jit(_take)/gather | solution.py:62
  162.2 5.2 %gather_fusion.2 = f32[64,68,132]{1,2,0:T(8,128)} fusion(f32[64,68,132]{1,2,0:T(8,128)} %pad_maximum_fusion, s32[1024]{0:T(1024)S(1)} %get-tuple-element.143), kind=kCustom, calls=%fused_computation.2.clone | custom fusion | bytes 4595968 | tf_op jit(solution)/shard_map/jit(_take)/gather | solution.py:62
  167.4 5.2 %gather_fusion.3 = f32[64,68,132]{1,2,0:T(8,128)} fusion(f32[64,68,132]{1,2,0:T(8,128)} %pad_maximum_fusion, s32[1024]{0:T(1024)S(1)} %get-tuple-element.142), kind=kCustom, calls=%fused_computation.3.clone | custom fusion | bytes 4595968 | tf_op jit(solution)/shard_map/jit(_take)/gather | solution.py:62
  172.6 7.3 %fusion.21 = f32[64,68,132]{1,2,0:T(8,128)S(1)} fusion(f32[64,68,132]{1,2,0:T(8,128)} %gather_fusion.3, f32[64,68,132]{1,2,0:T(8,128)} %gather_fusion.2, f32[64,68,132]{1,2,0:T(8,128)} %gather_fusion.1, f32[64,68,132]{1,2,0:T(8,128)} %gather_fusion, f32[64]{0:T(128)S(1)} %get-tuple-element.114, f32[64]{0:T(128)S(1)} %get-tuple-element.115, ...), kind=kLoop, calls=%fused_computation.70 | loop fusion | flops 6319104 | bytes 11490560 | tf_op jit(solution)/shard_map/add | solution.py:62
  216.9 5.2 %gather_fusion.4 = f32[64,68,132]{1,2,0:T(8,128)} fusion(f32[64,68,132]{1,2,0:T(8,128)} %pad_maximum_fusion.1, s32[1024]{0:T(1024)S(1)} %get-tuple-element.149), kind=kCustom, calls=%fused_computation.4.clone | custom fusion | bytes 4595968 | tf_op jit(solution)/shard_map/jit(_take)/gather | solution.py:62
  222.1 5.1 %gather_fusion.5 = f32[64,68,132]{1,2,0:T(8,128)} fusion(f32[64,68,132]{1,2,0:T(8,128)} %pad_maximum_fusion.1, s32[1024]{0:T(1024)S(1)} %get-tuple-element.148), kind=kCustom, calls=%fused_computation.5.clone | custom fusion | bytes 4595968 | tf_op jit(solution)/shard_map/jit(_take)/gather | solution.py:62
  227.3 5.2 %gather_fusion.6 = f32[64,68,132]{1,2,0:T(8,128)} fusion(f32[64,68,132]{1,2,0:T(8,128)} %pad_maximum_fusion.1, s32[1024]{0:T(1024)S(1)} %get-tuple-element.147), kind=kCustom, calls=%fused_computation.6.clone | custom fusion | bytes 4595968 | tf_op jit(solution)/shard_map/jit(_take)/gather | solution.py:62
  232.5 5.2 %gather_fusion.7 = f32[64,68,132]{1,2,0:T(8,128)} fusion(f32[64,68,132]{1,2,0:T(8,128)} %pad_maximum_fusion.1, s32[1024]{0:T(1024)S(1)} %get-tuple-element.146), kind=kCustom, calls=%fused_computation.7.clone | custom fusion | bytes 4595968 | tf_op jit(solution)/shard_map/jit(_take)/gather | solution.py:62
  237.7 7.3 %fusion.18 = f32[64,68,132]{1,2,0:T(8,128)S(1)} fusion(f32[64,68,132]{1,2,0:T(8,128)} %gather_fusion.7, f32[64,68,132]{1,2,0:T(8,128)} %gather_fusion.6, f32[64,68,132]{1,2,0:T(8,128)} %gather_fusion.5, f32[64,68,132]{1,2,0:T(8,128)} %gather_fusion.4, f32[64]{0:T(128)S(1)} %get-tuple-element.102, f32[64]{0:T(128)S(1)} %get-tuple-element.103, ...), kind=kLoop, calls=%fused_computation.63 | loop fusion | flops 6319104 | bytes 11490560 | tf_op jit(solution)/shard_map/add | solution.py:62
  282.0 5.2 %gather_fusion.8 = f32[64,68,132]{1,2,0:T(8,128)} fusion(f32[64,68,132]{1,2,0:T(8,128)} %pad_maximum_fusion.2, s32[1024]{0:T(1024)S(1)} %get-tuple-element.153), kind=kCustom, calls=%fused_computation.8.clone | custom fusion | bytes 4595968 | tf_op jit(solution)/shard_map/jit(_take)/gather | solution.py:62
  292.4 5.2 %gather_fusion.10 = f32[64,68,132]{1,2,0:T(8,128)} fusion(f32[64,68,132]{1,2,0:T(8,128)} %pad_maximum_fusion.2, s32[1024]{0:T(1024)S(1)} %get-tuple-element.151), kind=kCustom, calls=%fused_computation.10.clone | custom fusion | bytes 4595968 | tf_op jit(solution)/shard_map/jit(_take)/gather | solution.py:62
  297.6 5.2 %gather_fusion.11 = f32[64,68,132]{1,2,0:T(8,128)} fusion(f32[64,68,132]{1,2,0:T(8,128)} %pad_maximum_fusion.2, s32[1024]{0:T(1024)S(1)} %get-tuple-element.150), kind=kCustom, calls=%fused_computation.11.clone | custom fusion | bytes 4595968 | tf_op jit(solution)/shard_map/jit(_take)/gather | solution.py:62
  302.8 7.3 %fusion.15 = f32[64,68,132]{1,2,0:T(8,128)S(1)} fusion(f32[64,68,132]{1,2,0:T(8,128)} %gather_fusion.11, f32[64,68,132]{1,2,0:T(8,128)} %gather_fusion.10, f32[64,68,132]{1,2,0:T(8,128)} %gather_fusion.9, f32[64,68,132]{1,2,0:T(8,128)} %gather_fusion.8, f32[64]{0:T(128)S(1)} %get-tuple-element.90, f32[64]{0:T(128)S(1)} %get-tuple-element.91, ...), kind=kLoop, calls=%fused_computation.56 | loop fusion | flops 6319104 | bytes 11490560 | tf_op jit(solution)/shard_map/add | solution.py:62
  347.2 5.1 %gather_fusion.12 = f32[64,68,132]{1,2,0:T(8,128)} fusion(f32[64,68,132]{1,2,0:T(8,128)} %pad_maximum_fusion.3, s32[1024]{0:T(1024)S(1)} %get-tuple-element.157), kind=kCustom, calls=%fused_computation.12.clone | custom fusion | bytes 4595968 | tf_op jit(solution)/shard_map/jit(_take)/gather | solution.py:62
  352.3 5.2 %gather_fusion.13 = f32[64,68,132]{1,2,0:T(8,128)} fusion(f32[64,68,132]{1,2,0:T(8,128)} %pad_maximum_fusion.3, s32[1024]{0:T(1024)S(1)} %get-tuple-element.156), kind=kCustom, calls=%fused_computation.13.clone | custom fusion | bytes 4595968 | tf_op jit(solution)/shard_map/jit(_take)/gather | solution.py:62
  357.6 5.2 %gather_fusion.14 = f32[64,68,132]{1,2,0:T(8,128)} fusion(f32[64,68,132]{1,2,0:T(8,128)} %pad_maximum_fusion.3, s32[1024]{0:T(1024)S(1)} %get-tuple-element.155), kind=kCustom, calls=%fused_computation.14.clone | custom fusion | bytes 4595968 | tf_op jit(solution)/shard_map/jit(_take)/gather | solution.py:62
  362.8 5.2 %gather_fusion.15 = f32[64,68,132]{1,2,0:T(8,128)} fusion(f32[64,68,132]{1,2,0:T(8,128)} %pad_maximum_fusion.3, s32[1024]{0:T(1024)S(1)} %get-tuple-element.154), kind=kCustom, calls=%fused_computation.15.clone | custom fusion | bytes 4595968 | tf_op jit(solution)/shard_map/jit(_take)/gather | solution.py:62
  368.1 7.3 %fusion.12 = f32[64,68,132]{1,2,0:T(8,128)S(1)} fusion(f32[64,68,132]{1,2,0:T(8,128)} %gather_fusion.15, f32[64,68,132]{1,2,0:T(8,128)} %gather_fusion.14, f32[64,68,132]{1,2,0:T(8,128)} %gather_fusion.13, f32[64,68,132]{1,2,0:T(8,128)} %gather_fusion.12, f32[64]{0:T(128)S(1)} %copy-done.25, f32[64]{0:T(128)S(1)} %copy-done.26, f32[64]{0:T(128)S(1)} %copy-done.24, ...), kind=kLoop, calls=%fused_computation.49 | loop fusion | flops 6319104 | bytes 11490560 | tf_op jit(solution)/shard_map/add | solution.py:62
  386.4 54.7 %all_to_all.36 = f32[64,128,64]{1,2,0:T(8,128)S(1)} all-to-all(f32[64,128,64]{1,2,0:T(8,128)S(1)} %copy.40), channel_id=1, replica_groups=mesh['gz'=8,'xy'=4] {'gz'}, dimensions={0} | all-to-all | bytes 4194304 | tf_op jit(solution)/shard_map/all_to_all | solution.py:70
  (181 shorter events, 166.9 us)
Async XLA Ops:
  0.0 109.7 %copy-start = (f32[16,3]{0,1:T(4,128)S(1)}, f32[16,3]{0,1:T(4,128)}, u32[]{:S(2)}) copy-start(f32[16,3]{0,1:T(4,128)} %param.9) | copy-start | bytes 580
  0.0 10.2 %copy-start.18 = (s32[4,8,1,4]{1,3,2,0:T(4,128)S(1)}, s32[4,8,1,4]{1,3,2,0:T(4,128)}, u32[]{:S(2)}) copy-start(s32[4,8,1,4]{1,3,2,0:T(4,128)} %param.8) | copy-start | bytes 1540
  0.0 10.4 %copy-start.19 = (s32[4,8,1,4]{1,3,2,0:T(4,128)S(1)}, s32[4,8,1,4]{1,3,2,0:T(4,128)}, u32[]{:S(2)}) copy-start(s32[4,8,1,4]{1,3,2,0:T(4,128)} %param.7) | copy-start | bytes 1540
  2.9 109.0 %all-to-all-start = ((f32[8,128,512]{1,0,2:T(8,128)}), f32[8,128,512]{1,0,2:T(8,128)S(1)}, u32[]{:S(2)}, u32[]{:S(2)}) async-start(f32[8,128,512]{1,0,2:T(8,128)} %copy.20), calls=%async_computation | async-start | bytes 4194304 | tf_op jit(solution)/shard_map/all_to_all | solution.py:39
  128.9 7.7 %collective-permute-start = (f32[64,2,128]{2,0,1:T(8,128)S(1)}, f32[64,2,128]{2,0,1:T(8,128)S(1)}, u32[]{:S(2)}, u32[]{:S(2)}) collective-permute-start(f32[64,2,128]{2,0,1:T(8,128)S(1)} %copy.24), channel_id=1, source_target_pairs={{0,4},{4,8},{8,12},{12,16},{16,20},{20,24},{24,28},{28,0},{1,5},{5... | collective-permute-start | bytes 196616 | tf_op jit(solution)/shard_map/ppermute | solution.py:14
  131.8 7.5 %collective-permute-start.1 = (f32[64,2,128]{2,0,1:T(8,128)S(1)}, f32[64,2,128]{2,0,1:T(8,128)S(1)}, u32[]{:S(2)}, u32[]{:S(2)}) collective-permute-start(f32[64,2,128]{2,0,1:T(8,128)S(1)} %copy.25), channel_id=1, source_target_pairs={{4,0},{8,4},{12,8},{16,12},{20,16},{24,20},{28,24},{0,28},{5,1},{9... | collective-permute-start | bytes 196616 | tf_op jit(solution)/shard_map/ppermute | solution.py:16
  143.8 3.7 collective-permute-start.2
  143.8 4.1 collective-permute-start.3
  194.3 7.7 %collective-permute-start.4 = (f32[64,2,128]{2,0,1:T(8,128)S(1)}, f32[64,2,128]{2,0,1:T(8,128)S(1)}, u32[]{:S(2)}, u32[]{:S(2)}) collective-permute-start(f32[64,2,128]{2,0,1:T(8,128)S(1)} %copy.28), channel_id=1, source_target_pairs={{0,4},{4,8},{8,12},{12,16},{16,20},{20,24},{24,28},{28,0},{1,5},{5... | collective-permute-start | bytes 196616 | tf_op jit(solution)/shard_map/ppermute | solution.py:14
  197.2 7.5 %collective-permute-start.5 = (f32[64,2,128]{2,0,1:T(8,128)S(1)}, f32[64,2,128]{2,0,1:T(8,128)S(1)}, u32[]{:S(2)}, u32[]{:S(2)}) collective-permute-start(f32[64,2,128]{2,0,1:T(8,128)S(1)} %copy.29), channel_id=1, source_target_pairs={{4,0},{8,4},{12,8},{16,12},{20,16},{24,20},{28,24},{0,28},{5,1},{9... | collective-permute-start | bytes 196616 | tf_op jit(solution)/shard_map/ppermute | solution.py:16
  209.2 3.7 collective-permute-start.6
  210.3 2.7 collective-permute-start.7
  259.3 7.7 %collective-permute-start.8 = (f32[64,2,128]{2,0,1:T(8,128)S(1)}, f32[64,2,128]{2,0,1:T(8,128)S(1)}, u32[]{:S(2)}, u32[]{:S(2)}) collective-permute-start(f32[64,2,128]{2,0,1:T(8,128)S(1)} %copy.32), channel_id=1, source_target_pairs={{0,4},{4,8},{8,12},{12,16},{16,20},{20,24},{24,28},{28,0},{1,5},{5... | collective-permute-start | bytes 196616 | tf_op jit(solution)/shard_map/ppermute | solution.py:14
  262.3 7.5 %collective-permute-start.9 = (f32[64,2,128]{2,0,1:T(8,128)S(1)}, f32[64,2,128]{2,0,1:T(8,128)S(1)}, u32[]{:S(2)}, u32[]{:S(2)}) collective-permute-start(f32[64,2,128]{2,0,1:T(8,128)S(1)} %copy.33), channel_id=1, source_target_pairs={{4,0},{8,4},{12,8},{16,12},{20,16},{24,20},{28,24},{0,28},{5,1},{9... | collective-permute-start | bytes 196616 | tf_op jit(solution)/shard_map/ppermute | solution.py:16
  274.3 3.7 collective-permute-start.10
  275.4 2.8 collective-permute-start.11
  321.6 10.5 %copy-start.38 = (s32[64]{0:T(128)S(1)}, s32[64]{0:T(128)}, u32[]{:S(2)}) copy-start(s32[64]{0:T(128)} %get-tuple-element.15) | copy-start | bytes 772
  321.6 10.5 %copy-start.39 = (s32[64]{0:T(128)S(1)}, s32[64]{0:T(128)}, u32[]{:S(2)}) copy-start(s32[64]{0:T(128)} %get-tuple-element.119) | copy-start | bytes 772
  324.5 7.7 %collective-permute-start.12 = (f32[64,2,128]{2,0,1:T(8,128)S(1)}, f32[64,2,128]{2,0,1:T(8,128)S(1)}, u32[]{:S(2)}, u32[]{:S(2)}) collective-permute-start(f32[64,2,128]{2,0,1:T(8,128)S(1)} %copy.36), channel_id=1, source_target_pairs={{0,4},{4,8},{8,12},{12,16},{16,20},{20,24},{24,28},{28,0},{1,5},{5... | collective-permute-start | bytes 196616 | tf_op jit(solution)/shard_map/ppermute | solution.py:14
  327.4 7.5 %collective-permute-start.13 = (f32[64,2,128]{2,0,1:T(8,128)S(1)}, f32[64,2,128]{2,0,1:T(8,128)S(1)}, u32[]{:S(2)}, u32[]{:S(2)}) collective-permute-start(f32[64,2,128]{2,0,1:T(8,128)S(1)} %copy.37), channel_id=1, source_target_pairs={{4,0},{8,4},{12,8},{16,12},{20,16},{24,20},{28,24},{0,28},{5,1},{9... | collective-permute-start | bytes 196616 | tf_op jit(solution)/shard_map/ppermute | solution.py:16
  339.4 3.7 collective-permute-start.14
  340.6 2.7 collective-permute-start.15
  368.1 7.3 %copy-start.32 = (f32[64]{0:T(128)S(1)}, f32[64]{0:T(128)}, u32[]{:S(2)}) copy-start(f32[64]{0:T(128)} %get-tuple-element.74) | copy-start | bytes 772
  386.4 56.7 %copy-start.1 = (f32[16,3]{0,1:T(4,128)S(1)}, f32[16,3]{0,1:T(4,128)}, u32[]{:S(2)}) copy-start(f32[16,3]{0,1:T(4,128)} %param.9) | copy-start | bytes 580
  (33 other events, 175.7 us)
where the time goes:
time: 449 us; the launch traced here: 443 us
  local copies, waits for them, and re-layouts  164 us (37%)
  blocking collectives  153 us (34%)
  other arithmetic  81.6 us (18%)
  starting transfers between devices  34.7 us (8%)
  waiting for transfers between devices  7.61 us (2%)
    gather x16, local copies, waits for them, and re-layouts, column_steps(): jnp.take(rimmed, source, axis=0)  83.1 us
    all_gather x1, blocking collectives, column_steps(): lax.all_gather(frac_index, 'gz', axis=1, tiled=True)  68.2 us
    all_to_all x1, blocking collectives, column_steps(): lax.all_to_all(jnp.swapaxes(standing, 1, 2), 'gz', split_axis=0, concat_a...  54.7 us
    slice x8, local copies, waits for them, and re-layouts, extended(): lax.slice_in_dim(cells, cells.shape[dim] - width, cells.shape[dim], axis=...  34 us
    all_gather x1, blocking collectives, column_steps(): lax.all_gather(offsets, 'gz', axis=1, tiled=True)  30.5 us
    add x4, other arithmetic, column_steps(): merged + zweights[node][:, None, None] * jnp.take(rimmed, source, axis=0)  29 us
    ppermute x8, starting transfers between devices, extended(): lax.ppermute(head, axis, [((i + 1) % count, i) for i in range(count)])  23.7 us
    add x4, other arithmetic, column_steps(): along_y + yweights[node][:, None, None] * merged[:, node:node + width_y, :]  17.9 us
  transfers between devices with their start and end apart: 17, of which 8 were waited for; matrix products, arithmetic and copies ran while one was open for 6% of the time, Pallas kernels for 0%

commit v1 on v0

--- a/solution.py
+++ b/solution.py
@@ -33,7 +33,7 @@
     step_count = offsets.shape[0]
     all_shifts, all_index = (
         lax.all_gather(offsets, "gz", axis=1, tiled=True),
-        lax.all_gather(frac_index, "gz", axis=1, tiled=True),
+        jnp.concatenate(lax.all_gather(frac_index, "gz"), axis=1),
     )
     standing = jnp.swapaxes(
         lax.all_to_all(image, "gz", split_axis=2, concat_axis=0, tiled=True), 1, 2

time: 449 us -> 449 us (level)
  no operation moved by 1% of the time
where the time goes in v1:
time: 449 us; the launch traced here: 444 us
  local copies, waits for them, and re-layouts  165 us (37%)
  blocking collectives  153 us (34%)
  other arithmetic  81.7 us (18%)
  starting transfers between devices  34.7 us (8%)
  waiting for transfers between devices  7.61 us (2%)
    gather x16, local copies, waits for them, and re-layouts, column_steps(): jnp.take(rimmed, source, axis=0)  83.1 us
    all_gather x1, blocking collectives, column_steps(): lax.all_gather(frac_index, 'gz')  68.3 us
    all_to_all x1, blocking collectives, column_steps(): lax.all_to_all(jnp.swapaxes(standing, 1, 2), 'gz', split_axis=0, concat_a...  54.7 us
    slice x8, local copies, waits for them, and re-layouts, extended(): lax.slice_in_dim(cells, cells.shape[dim] - width, cells.shape[dim], axis=...  34 us
    all_gather x1, blocking collectives, column_steps(): lax.all_gather(offsets, 'gz', axis=1, tiled=True)  30.5 us
    add x4, other arithmetic, column_steps(): merged + zweights[node][:, None, None] * jnp.take(rimmed, source, axis=0)  29 us
    ppermute x8, starting transfers between devices, extended(): lax.ppermute(head, axis, [((i + 1) % count, i) for i in range(count)])  23.7 us
    add x4, other arithmetic, column_steps(): along_y + yweights[node][:, None, None] * merged[:, node:node + width_y, :]  17.9 us
  transfers between devices with their start and end apart: 17, of which 8 were waited for; matrix products, arithmetic and copies ran while one was open for 6% of the time, Pallas kernels for 0%

profile of v1, /device:TPU:0, one launch (start us, length us, event | category | flops | bytes accessed | tf_op | source)
XLA Modules:
  0.0 443.7 jit_solution(11436704829284578045)
XLA Ops:
  2.9 7.3 %all-to-all-start = ((f32[8,128,512]{1,0,2:T(8,128)}), f32[8,128,512]{1,0,2:T(8,128)S(1)}, u32[]{:S(2)}, u32[]{:S(2)}) async-start(f32[8,128,512]{1,0,2:T(8,128)} %copy.15), calls=%async_computation | async-start | bytes 4194304 | tf_op jit(solution)/shard_map/all_to_all | solution.py:39
  10.4 68.3 %all-gather = s32[32,8,1,4]{1,3,2,0:T(4,128)S(1)} all-gather(s32[4,8,1,4]{1,3,2,0:T(4,128)S(1)} %copy-done.19), channel_id=2, replica_groups=mesh['gz'=8,'xy'=4] {'gz'}, dimensions={0}, use_global_device_ids=true | all-gather | bytes 4608 | tf_op jit(solution)/shard_map/all_gather | solution.py:36
  79.1 30.5 %all_gather.11 = s32[4,64,1,4]{3,0,2,1:T(4,128)S(1)} all-gather(s32[4,8,1,4]{3,0,2,1:T(4,128)S(1)} %copy.11), channel_id=1, replica_groups=mesh['gz'=8,'xy'=4] {'gz'}, dimensions={1}, use_global_device_ids=true | all-gather | bytes 4608 | tf_op jit(solution)/shard_map/all_gather | solution.py:35
  118.2 8.1 %fusion.164 = (f32[64,2,128]{1,2,0:T(8,128)}, f32[64,2,128]{1,2,0:T(8,128)}) fusion(f32[64,64,128]{1,2,0:T(8,128)} %bitcast.508), kind=kLoop, calls=%fused_computation.477 | loop fusion | bytes 262144 | tf_op jit(solution)/shard_map/slice | solution.py:11
  152.1 5.2 %gather_fusion = f32[64,68,132]{1,2,0:T(8,128)} fusion(f32[64,68,132]{1,2,0:T(8,128)} %pad_maximum_fusion, s32[1024]{0:T(1024)S(1)} %get-tuple-element.141), kind=kCustom, calls=%fused_computation.clone | custom fusion | bytes 4595968 | tf_op jit(solution)/shard_map/jit(_take)/gather | solution.py:62
  157.3 5.1 %gather_fusion.1 = f32[64,68,132]{1,2,0:T(8,128)} fusion(f32[64,68,132]{1,2,0:T(8,128)} %pad_maximum_fusion, s32[1024]{0:T(1024)S(1)} %get-tuple-element.140), kind=kCustom, calls=%fused_computation.1.clone | custom fusion | bytes 4595968 | tf_op jit(solution)/shard_map/jit(_take)/gather | solution.py:62
  162.5 5.2 %gather_fusion.2 = f32[64,68,132]{1,2,0:T(8,128)} fusion(f32[64,68,132]{1,2,0:T(8,128)} %pad_maximum_fusion, s32[1024]{0:T(1024)S(1)} %get-tuple-element.139), kind=kCustom, calls=%fused_computation.2.clone | custom fusion | bytes 4595968 | tf_op jit(solution)/shard_map/jit(_take)/gather | solution.py:62
  167.7 5.2 %gather_fusion.3 = f32[64,68,132]{1,2,0:T(8,128)} fusion(f32[64,68,132]{1,2,0:T(8,128)} %pad_maximum_fusion, s32[1024]{0:T(1024)S(1)} %get-tuple-element.138), kind=kCustom, calls=%fused_computation.3.clone | custom fusion | bytes 4595968 | tf_op jit(solution)/shard_map/jit(_take)/gather | solution.py:62
  172.9 7.3 %fusion.21 = f32[64,68,132]{1,2,0:T(8,128)S(1)} fusion(f32[64,68,132]{1,2,0:T(8,128)} %gather_fusion.3, f32[64,68,132]{1,2,0:T(8,128)} %gather_fusion.2, f32[64,68,132]{1,2,0:T(8,128)} %gather_fusion.1, f32[64,68,132]{1,2,0:T(8,128)} %gather_fusion, f32[64]{0:T(128)S(1)} %get-tuple-element.110, f32[64]{0:T(128)S(1)} %get-tuple-element.111, ...), kind=kLoop, calls=%fused_computation.70 | loop fusion | flops 6319104 | bytes 11490560 | tf_op jit(solution)/shard_map/add | solution.py:62
  217.2 5.2 %gather_fusion.4 = f32[64,68,132]{1,2,0:T(8,128)} fusion(f32[64,68,132]{1,2,0:T(8,128)} %pad_maximum_fusion.1, s32[1024]{0:T(1024)S(1)} %get-tuple-element.145), kind=kCustom, calls=%fused_computation.4.clone | custom fusion | bytes 4595968 | tf_op jit(solution)/shard_map/jit(_take)/gather | solution.py:62
  222.4 5.1 %gather_fusion.5 = f32[64,68,132]{1,2,0:T(8,128)} fusion(f32[64,68,132]{1,2,0:T(8,128)} %pad_maximum_fusion.1, s32[1024]{0:T(1024)S(1)} %get-tuple-element.144), kind=kCustom, calls=%fused_computation.5.clone | custom fusion | bytes 4595968 | tf_op jit(solution)/shard_map/jit(_take)/gather | solution.py:62
  227.5 5.2 %gather_fusion.6 = f32[64,68,132]{1,2,0:T(8,128)} fusion(f32[64,68,132]{1,2,0:T(8,128)} %pad_maximum_fusion.1, s32[1024]{0:T(1024)S(1)} %get-tuple-element.143), kind=kCustom, calls=%fused_computation.6.clone | custom fusion | bytes 4595968 | tf_op jit(solution)/shard_map/jit(_take)/gather | solution.py:62
  232.8 5.2 %gather_fusion.7 = f32[64,68,132]{1,2,0:T(8,128)} fusion(f32[64,68,132]{1,2,0:T(8,128)} %pad_maximum_fusion.1, s32[1024]{0:T(1024)S(1)} %get-tuple-element.142), kind=kCustom, calls=%fused_computation.7.clone | custom fusion | bytes 4595968 | tf_op jit(solution)/shard_map/jit(_take)/gather | solution.py:62
  238.0 7.3 %fusion.18 = f32[64,68,132]{1,2,0:T(8,128)S(1)} fusion(f32[64,68,132]{1,2,0:T(8,128)} %gather_fusion.7, f32[64,68,132]{1,2,0:T(8,128)} %gather_fusion.6, f32[64,68,132]{1,2,0:T(8,128)} %gather_fusion.5, f32[64,68,132]{1,2,0:T(8,128)} %gather_fusion.4, f32[64]{0:T(128)S(1)} %get-tuple-element.98, f32[64]{0:T(128)S(1)} %get-tuple-element.99, ...), kind=kLoop, calls=%fused_computation.63 | loop fusion | flops 6319104 | bytes 11490560 | tf_op jit(solution)/shard_map/add | solution.py:62
  282.3 5.2 %gather_fusion.8 = f32[64,68,132]{1,2,0:T(8,128)} fusion(f32[64,68,132]{1,2,0:T(8,128)} %pad_maximum_fusion.2, s32[1024]{0:T(1024)S(1)} %get-tuple-element.149), kind=kCustom, calls=%fused_computation.8.clone | custom fusion | bytes 4595968 | tf_op jit(solution)/shard_map/jit(_take)/gather | solution.py:62
  292.6 5.2 %gather_fusion.10 = f32[64,68,132]{1,2,0:T(8,128)} fusion(f32[64,68,132]{1,2,0:T(8,128)} %pad_maximum_fusion.2, s32[1024]{0:T(1024)S(1)} %get-tuple-element.147), kind=kCustom, calls=%fused_computation.10.clone | custom fusion | bytes 4595968 | tf_op jit(solution)/shard_map/jit(_take)/gather | solution.py:62
  297.9 5.2 %gather_fusion.11 = f32[64,68,132]{1,2,0:T(8,128)} fusion(f32[64,68,132]{1,2,0:T(8,128)} %pad_maximum_fusion.2, s32[1024]{0:T(1024)S(1)} %get-tuple-element.146), kind=kCustom, calls=%fused_computation.11.clone | custom fusion | bytes 4595968 | tf_op jit(solution)/shard_map/jit(_take)/gather | solution.py:62
  303.1 7.3 %fusion.15 = f32[64,68,132]{1,2,0:T(8,128)S(1)} fusion(f32[64,68,132]{1,2,0:T(8,128)} %gather_fusion.11, f32[64,68,132]{1,2,0:T(8,128)} %gather_fusion.10, f32[64,68,132]{1,2,0:T(8,128)} %gather_fusion.9, f32[64,68,132]{1,2,0:T(8,128)} %gather_fusion.8, f32[64]{0:T(128)S(1)} %get-tuple-element.86, f32[64]{0:T(128)S(1)} %get-tuple-element.87, ...), kind=kLoop, calls=%fused_computation.56 | loop fusion | flops 6319104 | bytes 11490560 | tf_op jit(solution)/shard_map/add | solution.py:62
  347.4 5.1 %gather_fusion.12 = f32[64,68,132]{1,2,0:T(8,128)} fusion(f32[64,68,132]{1,2,0:T(8,128)} %pad_maximum_fusion.3, s32[1024]{0:T(1024)S(1)} %get-tuple-element.153), kind=kCustom, calls=%fused_computation.12.clone | custom fusion | bytes 4595968 | tf_op jit(solution)/shard_map/jit(_take)/gather | solution.py:62
  352.6 5.2 %gather_fusion.13 = f32[64,68,132]{1,2,0:T(8,128)} fusion(f32[64,68,132]{1,2,0:T(8,128)} %pad_maximum_fusion.3, s32[1024]{0:T(1024)S(1)} %get-tuple-element.152), kind=kCustom, calls=%fused_computation.13.clone | custom fusion | bytes 4595968 | tf_op jit(solution)/shard_map/jit(_take)/gather | solution.py:62
  357.8 5.2 %gather_fusion.14 = f32[64,68,132]{1,2,0:T(8,128)} fusion(f32[64,68,132]{1,2,0:T(8,128)} %pad_maximum_fusion.3, s32[1024]{0:T(1024)S(1)} %get-tuple-element.151), kind=kCustom, calls=%fused_computation.14.clone | custom fusion | bytes 4595968 | tf_op jit(solution)/shard_map/jit(_take)/gather | solution.py:62
  363.1 5.2 %gather_fusion.15 = f32[64,68,132]{1,2,0:T(8,128)} fusion(f32[64,68,132]{1,2,0:T(8,128)} %pad_maximum_fusion.3, s32[1024]{0:T(1024)S(1)} %get-tuple-element.150), kind=kCustom, calls=%fused_computation.15.clone | custom fusion | bytes 4595968 | tf_op jit(solution)/shard_map/jit(_take)/gather | solution.py:62
  368.3 7.3 %fusion.12 = f32[64,68,132]{1,2,0:T(8,128)S(1)} fusion(f32[64,68,132]{1,2,0:T(8,128)} %gather_fusion.15, f32[64,68,132]{1,2,0:T(8,128)} %gather_fusion.14, f32[64,68,132]{1,2,0:T(8,128)} %gather_fusion.13, f32[64,68,132]{1,2,0:T(8,128)} %gather_fusion.12, f32[64]{0:T(128)S(1)} %copy-done.25, f32[64]{0:T(128)S(1)} %copy-done.26, f32[64]{0:T(128)S(1)} %copy-done.24, ...), kind=kLoop, calls=%fused_computation.49 | loop fusion | flops 6319104 | bytes 11490560 | tf_op jit(solution)/shard_map/add | solution.py:62
  386.7 54.7 %all_to_all.36 = f32[64,128,64]{1,2,0:T(8,128)S(1)} all-to-all(f32[64,128,64]{1,2,0:T(8,128)S(1)} %copy.35), channel_id=1, replica_groups=mesh['gz'=8,'xy'=4] {'gz'}, dimensions={0} | all-to-all | bytes 4194304 | tf_op jit(solution)/shard_map/all_to_all | solution.py:70
  (184 shorter events, 167.0 us)
Async XLA Ops:
  0.0 109.9 %copy-start = (f32[16,3]{0,1:T(4,128)S(1)}, f32[16,3]{0,1:T(4,128)}, u32[]{:S(2)}) copy-start(f32[16,3]{0,1:T(4,128)} %param.9) | copy-start | bytes 580
  0.0 10.2 %copy-start.18 = (s32[4,8,1,4]{1,3,2,0:T(4,128)S(1)}, s32[4,8,1,4]{1,3,2,0:T(4,128)}, u32[]{:S(2)}) copy-start(s32[4,8,1,4]{1,3,2,0:T(4,128)} %param.7) | copy-start | bytes 1540
  0.0 10.4 %copy-start.19 = (s32[4,8,1,4]{1,3,2,0:T(4,128)S(1)}, s32[4,8,1,4]{1,3,2,0:T(4,128)}, u32[]{:S(2)}) copy-start(s32[4,8,1,4]{1,3,2,0:T(4,128)} %param.8) | copy-start | bytes 1540
  2.9 109.2 %all-to-all-start = ((f32[8,128,512]{1,0,2:T(8,128)}), f32[8,128,512]{1,0,2:T(8,128)S(1)}, u32[]{:S(2)}, u32[]{:S(2)}) async-start(f32[8,128,512]{1,0,2:T(8,128)} %copy.15), calls=%async_computation | async-start | bytes 4194304 | tf_op jit(solution)/shard_map/all_to_all | solution.py:39
  129.1 7.7 %collective-permute-start = (f32[64,2,128]{2,0,1:T(8,128)S(1)}, f32[64,2,128]{2,0,1:T(8,128)S(1)}, u32[]{:S(2)}, u32[]{:S(2)}) collective-permute-start(f32[64,2,128]{2,0,1:T(8,128)S(1)} %copy.19), channel_id=1, source_target_pairs={{0,4},{4,8},{8,12},{12,16},{16,20},{20,24},{24,28},{28,0},{1,5},{5... | collective-permute-start | bytes 196616 | tf_op jit(solution)/shard_map/ppermute | solution.py:14
  132.0 7.5 %collective-permute-start.1 = (f32[64,2,128]{2,0,1:T(8,128)S(1)}, f32[64,2,128]{2,0,1:T(8,128)S(1)}, u32[]{:S(2)}, u32[]{:S(2)}) collective-permute-start(f32[64,2,128]{2,0,1:T(8,128)S(1)} %copy.20), channel_id=1, source_target_pairs={{4,0},{8,4},{12,8},{16,12},{20,16},{24,20},{28,24},{0,28},{5,1},{9... | collective-permute-start | bytes 196616 | tf_op jit(solution)/shard_map/ppermute | solution.py:16
  144.0 3.7 collective-permute-start.2
  144.1 4.1 collective-permute-start.3
  194.5 7.7 %collective-permute-start.4 = (f32[64,2,128]{2,0,1:T(8,128)S(1)}, f32[64,2,128]{2,0,1:T(8,128)S(1)}, u32[]{:S(2)}, u32[]{:S(2)}) collective-permute-start(f32[64,2,128]{2,0,1:T(8,128)S(1)} %copy.23), channel_id=1, source_target_pairs={{0,4},{4,8},{8,12},{12,16},{16,20},{20,24},{24,28},{28,0},{1,5},{5... | collective-permute-start | bytes 196616 | tf_op jit(solution)/shard_map/ppermute | solution.py:14
  197.4 7.5 %collective-permute-start.5 = (f32[64,2,128]{2,0,1:T(8,128)S(1)}, f32[64,2,128]{2,0,1:T(8,128)S(1)}, u32[]{:S(2)}, u32[]{:S(2)}) collective-permute-start(f32[64,2,128]{2,0,1:T(8,128)S(1)} %copy.24), channel_id=1, source_target_pairs={{4,0},{8,4},{12,8},{16,12},{20,16},{24,20},{28,24},{0,28},{5,1},{9... | collective-permute-start | bytes 196616 | tf_op jit(solution)/shard_map/ppermute | solution.py:16
  209.5 3.7 collective-permute-start.6
  210.6 2.7 collective-permute-start.7
  259.6 7.7 %collective-permute-start.8 = (f32[64,2,128]{2,0,1:T(8,128)S(1)}, f32[64,2,128]{2,0,1:T(8,128)S(1)}, u32[]{:S(2)}, u32[]{:S(2)}) collective-permute-start(f32[64,2,128]{2,0,1:T(8,128)S(1)} %copy.27), channel_id=1, source_target_pairs={{0,4},{4,8},{8,12},{12,16},{16,20},{20,24},{24,28},{28,0},{1,5},{5... | collective-permute-start | bytes 196616 | tf_op jit(solution)/shard_map/ppermute | solution.py:14
  262.5 7.5 %collective-permute-start.9 = (f32[64,2,128]{2,0,1:T(8,128)S(1)}, f32[64,2,128]{2,0,1:T(8,128)S(1)}, u32[]{:S(2)}, u32[]{:S(2)}) collective-permute-start(f32[64,2,128]{2,0,1:T(8,128)S(1)} %copy.28), channel_id=1, source_target_pairs={{4,0},{8,4},{12,8},{16,12},{20,16},{24,20},{28,24},{0,28},{5,1},{9... | collective-permute-start | bytes 196616 | tf_op jit(solution)/shard_map/ppermute | solution.py:16
  274.5 3.7 collective-permute-start.10
  275.7 2.8 collective-permute-start.11
  321.9 10.5 %copy-start.38 = (s32[64]{0:T(128)S(1)}, s32[64]{0:T(128)}, u32[]{:S(2)}) copy-start(s32[64]{0:T(128)} %get-tuple-element.15) | copy-start | bytes 772
  321.9 10.5 %copy-start.39 = (s32[64]{0:T(128)S(1)}, s32[64]{0:T(128)}, u32[]{:S(2)}) copy-start(s32[64]{0:T(128)} %get-tuple-element.115) | copy-start | bytes 772
  324.7 7.7 %collective-permute-start.12 = (f32[64,2,128]{2,0,1:T(8,128)S(1)}, f32[64,2,128]{2,0,1:T(8,128)S(1)}, u32[]{:S(2)}, u32[]{:S(2)}) collective-permute-start(f32[64,2,128]{2,0,1:T(8,128)S(1)} %copy.31), channel_id=1, source_target_pairs={{0,4},{4,8},{8,12},{12,16},{16,20},{20,24},{24,28},{28,0},{1,5},{5... | collective-permute-start | bytes 196616 | tf_op jit(solution)/shard_map/ppermute | solution.py:14
  327.6 7.5 %collective-permute-start.13 = (f32[64,2,128]{2,0,1:T(8,128)S(1)}, f32[64,2,128]{2,0,1:T(8,128)S(1)}, u32[]{:S(2)}, u32[]{:S(2)}) collective-permute-start(f32[64,2,128]{2,0,1:T(8,128)S(1)} %copy.32), channel_id=1, source_target_pairs={{4,0},{8,4},{12,8},{16,12},{20,16},{24,20},{28,24},{0,28},{5,1},{9... | collective-permute-start | bytes 196616 | tf_op jit(solution)/shard_map/ppermute | solution.py:16
  339.7 3.7 collective-permute-start.14
  340.9 2.7 collective-permute-start.15
  368.3 7.3 %copy-start.32 = (f32[64]{0:T(128)S(1)}, f32[64]{0:T(128)}, u32[]{:S(2)}) copy-start(f32[64]{0:T(128)} %get-tuple-element.70) | copy-start | bytes 772
  386.7 56.7 %copy-start.1 = (f32[16,3]{0,1:T(4,128)S(1)}, f32[16,3]{0,1:T(4,128)}, u32[]{:S(2)}) copy-start(f32[16,3]{0,1:T(4,128)} %param.9) | copy-start | bytes 580
  (33 other events, 175.7 us)
